TPU v7x, 64 devices: a 2x2x8 block of a 4x4x8 slice. The times are simulated.
64 devices in a mesh: dp: 4 (over x, y), ctx: 16 (over z, core).
Axes of the slice: x: 2, y: 2, z: 8, core: 2. Of those that a mesh axis runs over, the one named last changes fastest.
The devices are a block of a 4x4x8 slice.
Arguments:
- queries: bfloat16 [32, 4096, 4, 128], P('dp', 'ctx'), parts along dimension 0
- keys: bfloat16 [32, 4096, 1, 128], P('dp', 'ctx'), parts along dimension 0
- values: bfloat16 [32, 4096, 1, 128], P('dp', 'ctx'), parts along dimension 0
- grad_out: bfloat16 [32, 4096, 4, 128], P('dp', 'ctx'), parts along dimension 0
Outputs:
- output 1: bfloat16 [32, 4096, 4, 128], P('dp', 'ctx'), parts along dimension 0
- output 2: bfloat16 [32, 4096, 4, 128], P('dp', 'ctx'), parts along dimension 0
- output 3: bfloat16 [32, 4096, 1, 128], P('dp', 'ctx'), parts along dimension 0
- output 4: bfloat16 [32, 4096, 1, 128], P('dp', 'ctx'), parts along dimension 0
There are 4 independent parts. A program takes and returns all parts, laid end to end along the dimension named above; each array names one.
All inputs are finite; a program needn't handle non-finite values.
Results may differ from a plain program's by a relative error of at most 0.00597021.
Values are sent between devices in bfloat16 or wider.
A program may use at most 768 MiB of HBM per device.

v0:
```python
import jax
import jax.numpy as jnp
from jax import lax
from jax.sharding import PartitionSpec as P

NEG_BIG = -1e30


def block_scores(q_heads, k_blk, q_start, k_start, scale):
    scores = jnp.einsum("bihgd,bjhd->bhgij", q_heads, k_blk, preferred_element_type=jnp.float32) * scale
    q_pos = q_start + jnp.arange(q_heads.shape[1])
    k_pos = k_start + jnp.arange(k_blk.shape[1])
    return jnp.where(q_pos[:, None] >= k_pos[None, :], scores, NEG_BIG)


def attend_forward(q_heads, k_all, v_all, dev_idx, scale):
    n_batch, c_len, n_kv, n_grp, d_head = q_heads.shape
    stat_shape = (n_batch, n_kv, n_grp, c_len)
    q_start = dev_idx * c_len

    def loop_body(key_idx, carry):
        m_run, l_run, acc_run = carry
        k_blk = lax.dynamic_index_in_dim(k_all, key_idx, 1, keepdims=False)
        v_blk = lax.dynamic_index_in_dim(v_all, key_idx, 1, keepdims=False)
        scores = block_scores(q_heads, k_blk, q_start, key_idx * c_len, scale)
        m_new = jnp.maximum(m_run, scores.max(axis=-1))
        rescale = jnp.exp(m_run - m_new)
        weights = jnp.exp(scores - m_new[..., None])
        l_new = l_run * rescale + weights.sum(axis=-1)
        acc_new = acc_run * rescale[..., None] + jnp.einsum("bhgij,bjhd->bhgid", weights.astype(jnp.bfloat16), v_blk, preferred_element_type=jnp.float32)
        return m_new, l_new, acc_new

    init_carry = (jnp.full(stat_shape, NEG_BIG, jnp.float32), jnp.zeros(stat_shape, jnp.float32), jnp.zeros(stat_shape + (d_head,), jnp.float32))
    m_fin, l_fin, acc_fin = lax.fori_loop(0, dev_idx + 1, loop_body, init_carry)
    out_heads = jnp.transpose((acc_fin / l_fin[..., None]).astype(jnp.bfloat16), (0, 3, 1, 2, 4))
    return out_heads, m_fin + jnp.log(l_fin)


def attend_backward(q_heads, do_heads, out_heads, lse_row, k_all, v_all, dev_idx, scale):
    c_len = q_heads.shape[1]
    q_start = dev_idx * c_len
    delta_row = jnp.einsum("bihgd,bihgd->bhgi", do_heads, out_heads, preferred_element_type=jnp.float32)

    def loop_body(key_idx, carry):
        dq_acc, dk_all, dv_all = carry
        k_blk = lax.dynamic_index_in_dim(k_all, key_idx, 1, keepdims=False)
        v_blk = lax.dynamic_index_in_dim(v_all, key_idx, 1, keepdims=False)
        scores = block_scores(q_heads, k_blk, q_start, key_idx * c_len, scale)
        weights = jnp.exp(scores - lse_row[..., None])
        dv_blk = jnp.einsum("bhgij,bihgd->bjhd", weights.astype(jnp.bfloat16), do_heads, preferred_element_type=jnp.float32)
        dp_blk = jnp.einsum("bihgd,bjhd->bhgij", do_heads, v_blk, preferred_element_type=jnp.float32)
        ds_half = (weights * (dp_blk - delta_row[..., None])).astype(jnp.bfloat16)
        dq_acc = dq_acc + jnp.einsum("bhgij,bjhd->bihgd", ds_half, k_blk, preferred_element_type=jnp.float32)
        dk_blk = jnp.einsum("bhgij,bihgd->bjhd", ds_half, q_heads, preferred_element_type=jnp.float32)
        dk_all = lax.dynamic_update_index_in_dim(dk_all, dk_blk, key_idx, 1)
        dv_all = lax.dynamic_update_index_in_dim(dv_all, dv_blk, key_idx, 1)
        return dq_acc, dk_all, dv_all

    acc_zero = jnp.zeros(k_all.shape, jnp.float32)
    init_carry = (jnp.zeros(q_heads.shape, jnp.float32), acc_zero, acc_zero)
    return lax.fori_loop(0, dev_idx + 1, loop_body, init_carry)


def solution(mesh):
    part_spec = P("dp", "ctx")

    def local_step(queries, keys, values, grad_out):
        n_batch, c_len, n_q, d_head = queries.shape
        n_kv = keys.shape[2]
        scale = d_head ** -0.5
        dev_idx = lax.axis_index("ctx")
        head_shape = (n_batch, c_len, n_kv, n_q // n_kv, d_head)
        q_heads = queries.reshape(head_shape)
        do_heads = grad_out.reshape(head_shape)
        k_all = lax.all_gather(keys, "ctx", axis=1)
        v_all = lax.all_gather(values, "ctx", axis=1)
        out_heads, lse_row = attend_forward(q_heads, k_all, v_all, dev_idx, scale)
        dq_acc, dk_all, dv_all = attend_backward(q_heads, do_heads, out_heads, lse_row, k_all, v_all, dev_idx, scale)
        dk_sum = lax.psum_scatter(dk_all, "ctx", scatter_dimension=1)
        dv_sum = lax.psum_scatter(dv_all, "ctx", scatter_dimension=1)
        attn_out = out_heads.reshape(n_batch, c_len, n_q, d_head)
        grad_q = (dq_acc * scale).astype(jnp.bfloat16).reshape(n_batch, c_len, n_q, d_head)
        grad_k = (dk_sum * scale).astype(jnp.bfloat16)
        grad_v = dv_sum.astype(jnp.bfloat16)
        return attn_out, grad_q, grad_k, grad_v

    return jax.shard_map(local_step, mesh=mesh, in_specs=(part_spec,) * 4, out_specs=(part_spec,) * 4, check_vma=False)
```

profile of v0, /device:TPU:21, one launch (start us, length us, event | category | flops | bytes accessed | tf_op | source)
XLA Modules:
  0.0 779.1 jit_solution(12668955399934666256)
XLA Ops:
  8.9 4.6 copy_bitcast_fusion
  13.5 53.7 %all-gather.5.cloned.1.call-done = bf16[8,4096,1,128]{3,1,0,2:T(8,128)(2,1)} async-done(((bf16[8,256,1,128]{3,1,0,2:T(8,128)(2,1)}), bf16[8,4096,1,128]{3,1,0,2:T(8,128)(2,1)}) %all-gather.5.cloned.1.call-update) | async-done | bytes 8388624 | tf_op jit(solution)/shard_map/all_gather | solution.py:75
  67.2 7.7 copy.22
  74.9 45.0 %all-gather.7.cloned.1.call-done = bf16[8,4096,1,128]{3,1,0,2:T(8,128)(2,1)} async-done(((bf16[8,256,1,128]{3,1,0,2:T(8,128)(2,1)}), bf16[8,4096,1,128]{3,1,0,2:T(8,128)(2,1)}) %all-gather.7.cloned.1.call-update) | async-done | bytes 8388624 | tf_op jit(solution)/shard_map/all_gather | solution.py:76
  119.9 7.7 copy.23
  127.6 2.4 broadcast_in_dim.47
  130.1 22.1 %while.28 = (s32[]{:T(128)}, f32[8,1,4,256]{3,2,0,1:T(4,128)S(1)}, f32[8,1,4,256]{3,2,0,1:T(4,128)S(1)}, f32[8,1,4,256,128]{4,3,2,0,1:T(8,128)}, s32[]{:T(128)},...) while((s32[]{:T(128)}, f32[8,1,4,256]{3,2,0,1:T(4,128)S(1)}, ...), condition=%wide.region_3.4_spmd, body=%wide.region_0.3_spmd.sunk | while | flops 1098998272 | bytes 71045368 | solution.py:34
  130.2 2.6 fusion.96
  134.7 4.5 bitcast_add_fusion.7
  141.2 2.6 fusion.96
  145.7 4.5 bitcast_add_fusion.7
  153.5 31.2 %fusion.69 = (f32[8,4,256]{1,2,0:T(8,128)S(1)}, bf16[8,1,4,256,128]{4,2,3,0,1:T(4,128)(2,1)}) fusion(bf16[8,256,4,128]{3,2,1,0:T(4,128)(2,1)} %param.11, f32[8,4,256]{1,2,0:T(8,128)} %copy.24, f32[8,1,4,256,128]{4,3,2,0,1:T(8,128)} %get-tuple-element.119), kind=kLoop, calls=%fused_computation.70 | loop fusion | flops 6283264 | bytes 8454144
  185.0 2.5 broadcast_in_dim.48
  187.6 7.8 %broadcast_in_dim.49.clone = f32[8,16,256,1,128]{4,2,0,3,1:T(8,128)} broadcast(f32[]{:T(128)} %constant.55.clone.1), dimensions={} | broadcast | bytes 16777220 | tf_op jit(solution)/shard_map/broadcast_in_dim | solution.py:59
  195.4 7.9 %broadcast_in_dim.49 = f32[8,16,256,1,128]{4,2,0,3,1:T(8,128)} broadcast(f32[]{:T(128)} %constant.55.clone.1), dimensions={} | broadcast | bytes 16777220 | tf_op jit(solution)/shard_map/broadcast_in_dim | solution.py:59
  203.3 27.7 %while.29 = (s32[]{:T(128)}, f32[8,256,1,4,128]{1,4,3,0,2:T(8,128)}, f32[8,16,256,1,128]{4,2,0,3,1:T(8,128)}, f32[8,16,256,1,128]{4,2,0,3,1:T(8,128)}, s32[]{:T(...) while((s32[]{:T(128)}, ...), condition=%wide.region_5.6_spmd, body=%wide.region_4.5_spmd.sunk | while | flops 2706440704 | bytes 100438328 | solution.py:61
  203.4 2.4 fusion.109
  205.9 3.7 fusion.110
  209.6 2.2 bitcast_add_fusion.8
  211.8 3.1 fusion.112
  214.9 2.2 fusion.111
  217.2 2.4 fusion.109
  219.7 3.7 fusion.110
  223.4 2.2 bitcast_add_fusion.8
  225.6 3.1 fusion.112
  228.7 2.3 fusion.111
  231.7 2.8 multiply_convert_fusion
  234.4 2.5 copy.49
  236.9 435.4 %reduce-scatter.5.cloned.1.call-done = f32[8,1,256,1,128]{4,2,0,3,1:T(8,128)} async-done(((f32[8,16,256,1,128]{4,2,0,3,1:T(8,128)}), f32[8,1,256,1,128]{4,2,0,3,1:T(8,128)}) %reduce-scatter.5.cloned.1.call-update) | async-done | bytes 1048592 | tf_op jit(solution)/shard_map/reduce_scatter | solution.py:80
  672.3 2.1 convert_bitcast_fusion
  674.4 96.1 %reduce-scatter.3.cloned.1.call-done = f32[8,1,256,1,128]{4,2,0,3,1:T(8,128)} async-done(((f32[8,16,256,1,128]{4,2,0,3,1:T(8,128)}), f32[8,1,256,1,128]{4,2,0,3,1:T(8,128)}) %reduce-scatter.3.cloned.1.call-update) | async-done | bytes 1048592 | tf_op jit(solution)/shard_map/reduce_scatter | solution.py:79
  770.5 2.1 fusion.71
  (49 shorter events, 12.1 us)
Async XLA Ops:
  7.2 60.0 %all-gather.5.cloned.1.call-start = ((), (), s32[]{:S(2)}) async-start(), calls=%async_computation.4 | async-start | bytes 8912896 | tf_op jit(solution)/shard_map/all_gather | solution.py:75
  8.0 112.0 %all-gather.7.cloned.1.call-start = ((), (), s32[]{:S(2)}) async-start(), calls=%async_computation.5 | async-start | bytes 8912896 | tf_op jit(solution)/shard_map/all_gather | solution.py:76
  8.8 663.5 %reduce-scatter.5.cloned.1.call-start = ((), (), s32[]{:S(2)}) async-start(), calls=%async_computation.3 | async-start | bytes 17825792 | tf_op jit(solution)/shard_map/reduce_scatter | solution.py:80
  130.2 4.5 copy-start.2
  139.2 1.9 copy-start.3
  141.2 4.5 copy-start.2
  150.2 1.9 copy-start.3
  203.3 2.6 copy-start.4
  205.8 3.7 copy-start
  211.8 5.3 copy-start.1
  217.1 2.6 copy-start.4
  219.6 3.7 copy-start
  225.6 5.4 copy-start.1
  231.0 539.4 %reduce-scatter.3.cloned.1.call-start = ((), (), s32[]{:S(2)}) async-start(), calls=%async_computation.2 | async-start | bytes 17825792 | tf_op jit(solution)/shard_map/reduce_scatter | solution.py:79
Sparse Core Ops, SparseCore 0:
  9.7 57.5 all-gather.4
  68.9 51.0 all-gather.6
  231.1 441.0 reduce-scatter.4
  674.5 95.9 reduce-scatter.2
where the time goes:
time: 781 us; the launch traced here: 779 us
  waiting for transfers between devices  632 us (81%)
  local copies, waits for them, and re-layouts  48.6 us (6%)
  other arithmetic  42.5 us (5%)
  matrix products  41.4 us (5%)
  between operations  13.8 us (2%)
    reduce_scatter x1, waiting for transfers between devices, local_step(): dv_sum = lax.psum_scatter(dv_all, 'ctx', scatter_dimension=1)  435 us
    reduce_scatter x1, waiting for transfers between devices, local_step(): dk_sum = lax.psum_scatter(dk_all, 'ctx', scatter_dimension=1)  96.1 us
    all_gather x1, waiting for transfers between devices, local_step(): k_all = lax.all_gather(keys, 'ctx', axis=1)  53.7 us
    all_gather x1, waiting for transfers between devices, local_step(): v_all = lax.all_gather(values, 'ctx', axis=1)  45 us
    unnamed x1, other arithmetic  31.2 us
    broadcast_in_dim x2, local copies, waits for them, and re-layouts, attend_backward(): acc_zero = jnp.zeros(k_all.shape, jnp.float32)  15.7 us
  transfers between devices with their start and end apart: 4, of which 4 were waited for; matrix products, arithmetic and copies ran while one was open for 3% of the time, Pallas kernels for 0%

commit v1 on v0

v1 whole, which is shorter than its diff:
```python
import functools
import math

import jax
import jax.numpy as jnp
from jax import lax
from jax.experimental import pallas as pl
from jax.experimental.pallas import tpu as pltpu
from jax.sharding import PartitionSpec as P

MESH = pl.DeviceIdType.MESH
NEG_BIG = -1e30
NT = (((1,), (1,)), ((), ()))
F32 = jnp.float32
BF16 = jnp.bfloat16


def dot(a, b):
    return jnp.dot(a, b, preferred_element_type=F32)


def dot_nt(a, b):
    return lax.dot_general(a, b, NT, preferred_element_type=F32)


def kernel(n_chip, n_grp, scale, q_ref, do_ref, k_ref, v_ref, o_ref, dq_ref, dkv_ref,
           q_in, do_in, kv, kt, vt, acc, part, o_st, dq_st, fin, s_buf, o_acc, dq_acc,
           send, recv, self_sem):
    n_dev = 2 * n_chip
    me = lax.axis_index("ctx")
    chip, core = me // 2, me % 2
    mate = 2 * chip + 1 - core
    c_len = kv.shape[2]
    rows = q_in.shape[1]
    half = rows // n_grp
    scale2 = scale * math.log2(math.e)

    barrier = pltpu.get_barrier_semaphore()

    def greet(s, _):
        pl.semaphore_signal(barrier, inc=1, device_id={"ctx": lax.rem(me + s, n_dev)}, device_id_type=MESH)
        return 0

    lax.fori_loop(1, n_dev, greet, 0)
    pl.semaphore_wait(barrier, n_dev - 1)

    def far_chip(n, sign):
        step = (2 * lax.rem(n, 2) - 1) * ((n + 1) // 2)
        return lax.rem(chip + sign * step + n_chip, n_chip)

    def remote(src, dst, kind, s_idx, r_idx, dev):
        return pltpu.make_async_remote_copy(src_ref=src, dst_ref=dst, send_sem=send.at[kind, s_idx], recv_sem=recv.at[kind, r_idx],
                                            device_id={"ctx": dev}, device_id_type=MESH)

    def q_copy(c, h):
        return remote(q_ref.at[c, h], q_in.at[me], 0, 2 * c + h, me, 2 * c + h)

    def do_copy(c, h):
        return remote(do_ref.at[c, h], do_in.at[me], 1, 2 * c + h, me, 2 * c + h)

    def kv_copy(c, h):
        return remote((k_ref, v_ref)[h].at[c], kv.at[h, me], 2, 2 * c + h, me, 2 * c + h)

    def fw_copy(i):
        return remote(kv.at[core, i], kv.at[core, i], 3, i, i, mate)

    def o_copy(i):
        return remote(o_st.at[i], o_ref.at[chip, core], 4, i, me, i)

    def dq_copy(i):
        return remote(dq_st.at[i], dq_ref.at[chip, core], 5, i, me, i)

    def fin_copy(i):
        return remote(fin.at[i], dkv_ref.at[core, chip], 6, i, me, i)

    part_copy = remote(acc.at[1 - core], part, 7, 0, 0, mate)

    def landed(dst, kind, i):
        return remote(dst, dst, kind, i, i, mate)

    def own(h):
        return (pltpu.make_async_copy(q_ref.at[chip, h], q_in.at[me], self_sem.at[0]),
                pltpu.make_async_copy(do_ref.at[chip, h], do_in.at[me], self_sem.at[1]),
                pltpu.make_async_copy((k_ref, v_ref)[h].at[chip], kv.at[h, me], self_sem.at[2]))

    for h in range(2):
        @pl.when(core == h)
        def _():
            kv_copy(chip, 1 - h).start()
            for cp in own(h):
                cp.start()

    def send_kv(n, _):
        c = far_chip(n, 1)
        for h in range(2):
            kv_copy(c, h).start()
        return 0

    lax.fori_loop(1, n_chip, send_kv, 0)

    for h in range(2):
        @pl.when(core == h)
        def _():
            q_copy(chip, 1 - h).start()
            do_copy(chip, 1 - h).start()

    def send_q(n, _):
        c = far_chip(n, 1)
        for h in range(2):
            q_copy(c, h).start()
            do_copy(c, h).start()
        return 0

    lax.fori_loop(1, n_chip, send_q, 0)

    acc[...] = jnp.zeros(acc.shape, F32)

    for h in range(2):
        @pl.when(core == h)
        def _():
            for cp in own(h):
                cp.wait()

    def source(n):
        return 2 * far_chip(n // 2, -1) + lax.rem(n, 2)

    def hand_over(n, _):
        i = source(n)

        @pl.when(i != me)
        def _():
            landed(kv.at[core, i], 2, i).wait_recv()

        fw_copy(i).start()
        return 0

    lax.fori_loop(0, n_dev, hand_over, 0)

    def turn(i, _):
        landed(kv.at[1 - core, i], 3, i).wait_recv()
        kt[i] = kv[0, i].astype(F32).T.astype(BF16)
        vt[i] = kv[1, i].astype(F32).T.astype(BF16)
        return 0

    lax.fori_loop(0, n_dev, turn, 0)

    def tile(n, _):
        i = source(n)

        @pl.when(i != me)
        def _():
            landed(q_in.at[i], 0, i).wait_recv()
            landed(do_in.at[i], 1, i).wait_recv()

        key_pos = lax.broadcasted_iota(jnp.int32, (c_len, rows), 0)
        q_pos = lax.broadcasted_iota(jnp.int32, (c_len, rows), 1) // n_grp + core * half
        x = jnp.where(key_pos <= q_pos, dot_nt(kv[0, i], q_in[i]) * scale2, NEG_BIG)
        s_buf[i] = x
        m = jnp.max(x, axis=0, keepdims=True)
        p = jnp.exp2(x - m)
        l = jnp.sum(p, axis=0, keepdims=True)
        o_acc[...] = dot(vt[i], p.astype(BF16))

        def forward(j, carry):
            m, l = carry
            x = dot_nt(kv[0, j], q_in[i]) * scale2
            s_buf[j] = x
            m_new = jnp.maximum(m, jnp.max(x, axis=0, keepdims=True))
            a = jnp.exp2(m - m_new)
            p = jnp.exp2(x - m_new)
            l = l * a + jnp.sum(p, axis=0, keepdims=True)
            o_acc[...] = o_acc[...] * a + dot(vt[j], p.astype(BF16))
            return m_new, l

        m, l = lax.fori_loop(0, i, forward, (m, l))
        o_half = (o_acc[...] * (1.0 / l)).astype(BF16)
        o_full = o_half.astype(F32)
        o_st[i] = o_full.T.astype(BF16)
        lse = m + jnp.log2(l)
        delta = jnp.sum(do_in[i].astype(F32).T * o_full, axis=0, keepdims=True)
        dq_acc[...] = jnp.zeros(dq_acc.shape, F32)

        @pl.when(i != me)
        def _():
            o_copy(i).start()

        def backward(j, _):
            p = jnp.exp2(s_buf[j] - lse)
            dp = dot_nt(kv[1, j], do_in[i])
            ds = (p * (dp - delta)).astype(BF16)
            acc[1, j] += dot(p.astype(BF16), do_in[i])
            acc[0, j] += dot(ds, q_in[i])
            dq_acc[...] += dot(kt[j], ds)
            return 0

        lax.fori_loop(0, i + 1, backward, 0)
        dq_st[i] = (dq_acc[...] * scale).T.astype(BF16)

        @pl.when(i != me)
        def _():
            dq_copy(i).start()

        return 0

    lax.fori_loop(0, n_dev, tile, 0)

    own_o = pltpu.make_async_copy(o_st.at[me], o_ref.at[chip, core], self_sem.at[3])
    own_dq = pltpu.make_async_copy(dq_st.at[me], dq_ref.at[chip, core], self_sem.at[4])
    own_fin = pltpu.make_async_copy(fin.at[me], dkv_ref.at[core, chip], self_sem.at[5])
    own_o.start()
    own_dq.start()

    part_copy.start()
    part_copy.wait()
    factor = jnp.where(core == 0, scale, 1.0).astype(F32)

    def finish(n, _):
        i = source(n)
        fin[i] = ((acc[core, i] + part[i]) * factor).astype(BF16)

        @pl.when(i != me)
        def _():
            fin_copy(i).start()

        return 0

    lax.fori_loop(0, n_dev, finish, 0)
    own_fin.start()

    def drain_in(i, _):
        fw_copy(i).wait_send()

        @pl.when(i != me)
        def _():
            c, h = i // 2, lax.rem(i, 2)
            landed(q_in.at[i], 0, i).wait_send()
            landed(do_in.at[i], 1, i).wait_send()
            landed(kv.at[0, i], 2, i).wait_send()
            o_copy(i).wait_send()
            dq_copy(i).wait_send()
            fin_copy(i).wait_send()
            landed(o_ref.at[c, h], 4, i).wait_recv()
            landed(dq_ref.at[c, h], 5, i).wait_recv()
            landed(dkv_ref.at[h, c], 6, i).wait_recv()

        return 0

    lax.fori_loop(0, n_dev, drain_in, 0)
    own_o.wait()
    own_dq.wait()
    own_fin.wait()


def solution(mesh):
    part_spec = P("dp", "ctx")
    n_ctx = mesh.shape["ctx"]
    n_chip = n_ctx // 2

    def local_step(queries, keys, values, grad_out):
        n_batch, c_len, n_q, d_head = queries.shape
        assert keys.shape[2] == 1 and n_batch == n_chip
        rows = c_len * n_q // 2
        q_shape = (n_batch, 2, rows, d_head)
        kv_shape = (n_batch, c_len, d_head)
        hbm = pl.BlockSpec(memory_space=pl.ANY)
        vmem = pltpu.VMEM
        out, grad_q, grad_kv = pl.pallas_call(
            functools.partial(kernel, n_chip, n_q, d_head ** -0.5),
            out_shape=(jax.ShapeDtypeStruct(q_shape, BF16), jax.ShapeDtypeStruct(q_shape, BF16), jax.ShapeDtypeStruct((2,) + kv_shape, BF16)),
            in_specs=[hbm] * 4,
            out_specs=(hbm,) * 3,
            scratch_shapes=[
                vmem((n_ctx, rows, d_head), BF16),
                vmem((n_ctx, rows, d_head), BF16),
                vmem((2, n_ctx, c_len, d_head), BF16),
                vmem((n_ctx, d_head, c_len), BF16),
                vmem((n_ctx, d_head, c_len), BF16),
                vmem((2, n_ctx, c_len, d_head), F32),
                vmem((n_ctx, c_len, d_head), F32),
                vmem((n_ctx, rows, d_head), BF16),
                vmem((n_ctx, rows, d_head), BF16),
                vmem((n_ctx, c_len, d_head), BF16),
                vmem((n_ctx, c_len, rows), F32),
                vmem((d_head, rows), F32),
                vmem((d_head, rows), F32),
                pltpu.SemaphoreType.DMA((8, n_ctx)),
                pltpu.SemaphoreType.DMA((8, n_ctx)),
                pltpu.SemaphoreType.DMA((6,)),
            ],
            compiler_params=pltpu.CompilerParams(collective_id=0, has_side_effects=True, vmem_limit_bytes=60 * 2 ** 20),
        )(queries.reshape(q_shape), grad_out.reshape(q_shape), keys.reshape(kv_shape), values.reshape(kv_shape))
        return (out.reshape(queries.shape), grad_q.reshape(queries.shape), grad_kv[0].reshape(keys.shape), grad_kv[1].reshape(values.shape))

    return jax.shard_map(local_step, mesh=mesh, in_specs=(part_spec,) * 4, out_specs=(part_spec,) * 4, check_vma=False)
```

time: 781 us -> 248 us (0.32)
  waiting for transfers between devices: 632 us -> 0 us
  Pallas kernels: 0 us -> 241 us
  local copies, waits for them, and re-layouts: 48.6 us -> 6.09 us
  other arithmetic: 42.5 us -> 0 us
  matrix products: 41.4 us -> 0 us
  between operations: 13.8 us -> 0.65 us
    reduce_scatter x2 -> x0, waiting for transfers between devices: 531 us -> none  [the longest x1 435 us: local_step(): dv_sum = lax.psum_scatter(dv_all, 'ctx', scatter_dimension=1)]
    pallas_call x0 -> x1, Pallas kernels: none -> 241 us  [local_step(): pl.pallas_call(functools.partial(kernel, n_chip, n_q, d_head ** (-0.5)),...]
    all_gather x2 -> x0, waiting for transfers between devices: 98.8 us -> none  [the longest x1 53.7 us: local_step(): k_all = lax.all_gather(keys, 'ctx', axis=1)]
    dot_general x14 -> x0, matrix products: 41.4 us -> none  [the longest x4 9.97 us: block_scores(): jnp.einsum('bihgd,bjhd->bhgij', q_heads, k_blk, preferred_element_type=jn...]
    unnamed x1 -> x0, other arithmetic: 31.2 us -> none
    broadcast_in_dim x6 -> x0, local copies, waits for them, and re-layouts: 20.7 us -> none  [the longest x2 15.7 us: attend_backward(): acc_zero = jnp.zeros(k_all.shape, jnp.float32)]
    while x24 -> x0, local copies, waits for them, and re-layouts: 19.2 us -> none  [the longest x2 15.4 us: attend_forward(): m_fin, l_fin, acc_fin = lax.fori_loop(0, dev_idx + 1, loop_body, init_carry)]
  transfers between devices with their start and end apart: 4 -> 0, of which waited for: 4 -> 0; matrix products, arithmetic and copies ran while one was open for 3% -> 0% of each run, Pallas kernels for 0% -> 0%
where the time goes in v1:
time: 248 us; the launch traced here: 247 us
  Pallas kernels  241 us (97%)
  local copies, waits for them, and re-layouts  6.09 us (2%)
    pallas_call x1, Pallas kernels, local_step(): pl.pallas_call(functools.partial(kernel, n_chip, n_q, d_head ** (-0.5)),...  241 us
    unnamed x7, local copies, waits for them, and re-layouts  6.09 us

profile of v1, /device:TPU:21, one launch (start us, length us, event | category | flops | bytes accessed | tf_op | source)
XLA Modules:
  0.0 247.5 jit_solution(12187426071222119700)
XLA Ops:
  0.6 240.7 %shard_map.75 = (bf16[8,2,512,128]{3,2,1,0:T(8,128)(2,1)}, bf16[8,2,512,128]{3,2,1,0:T(8,128)(2,1)}, bf16[2,8,256,128]{3,2,1,0:T(8,128)(2,1)}) custom-call(bf16[8,2,512,128]{3,2,1,0:T(8,128)(2,1)} %bitcast.14, bf16[8,2,512,128]{3,2,1,0:T(8,128)(2,1)} %bitcast.15, bf16[8,256,128]{2,1,0:T(8,128)(2,1)} %bitcast.18, bf16[8,256,128]{2,1,0:T(8,128)(2,1)} %bitcast.19), custom_call_target="tpu_custom_call" | custom-call | tf_op jit(solution)/shard_map/pallas_call | solution.py:267
  241.4 0.0 copy-start.1
  241.4 2.4 slice_bitcast_fusion
  243.8 0.0 copy-done.1
  243.8 0.0 copy-start
  243.8 1.3 copy.12
  245.1 1.0 copy-done
  246.1 1.3 copy.13
Async XLA Ops:
  241.4 2.4 copy-start.1
  243.8 2.3 copy-start

commit v2 on v0

v2 whole, which is shorter than its diff:
```python
import functools
import math

import jax
import jax.numpy as jnp
from jax import lax
from jax.experimental import pallas as pl
from jax.experimental.pallas import tpu as pltpu
from jax.sharding import PartitionSpec as P

MESH = pl.DeviceIdType.MESH
NEG_BIG = -1e30
NT = (((1,), (1,)), ((), ()))
F32 = jnp.float32
BF16 = jnp.bfloat16
Q, DO, KV, RELAY, SHARE, O, DQ, FIN, PART, N_KIND = range(10)


def dot(a, b):
    return jnp.dot(a, b, preferred_element_type=F32)


def dot_nt(a, b):
    return lax.dot_general(a, b, NT, preferred_element_type=F32)


def kernel(n_chip, n_grp, scale, q_ref, do_ref, k_ref, v_ref, o_ref, dq_ref, dk_ref, dv_ref,
           q_in, do_in, kv, kt, vt, acc, part, cross, o_st, dq_st, fin, s_buf, o_acc, dq_acc,
           send, recv, self_sem):
    n_dev = 2 * n_chip
    n_far = n_chip // 2
    me = lax.axis_index("ctx")
    chip, core = me // 2, me % 2
    mate = 2 * chip + 1 - core
    d_head = q_in.shape[-1]
    cols, keys = q_in.shape[1] * q_in.shape[2], kv.shape[3] * kv.shape[4]
    scale2 = scale * math.log2(math.e)

    barrier = pltpu.get_barrier_semaphore()

    def greet(s, _):
        pl.semaphore_signal(barrier, inc=1, device_id={"ctx": lax.rem(me + s, n_dev)}, device_id_type=MESH)
        return 0

    lax.fori_loop(1, n_dev, greet, 0)
    pl.semaphore_wait(barrier, n_dev - 1)

    def wrap(c):
        return lax.rem(c + 2 * n_chip, n_chip)

    def sign(r):
        return 1 - 2 * r

    def seq(r, c):
        return wrap(c - r)

    def remote(src, dst, kind, s_idx, r_idx, dev):
        return pltpu.make_async_remote_copy(src_ref=src, dst_ref=dst, send_sem=send.at[kind, s_idx], recv_sem=recv.at[kind, r_idx],
                                            device_id={"ctx": dev}, device_id_type=MESH)

    def landed(dst, kind, i):
        return remote(dst, dst, kind, i, i, mate)

    def out_q(r, d, h, src, dst, kind):
        c = wrap(chip + sign(r) * d)
        slot = n_far * r + d
        return remote(src.at[seq(r, c), h], dst.at[slot, core], kind, 2 * slot + h, 2 * slot + core, 2 * c + h)

    def out_kv(r, d, h):
        c = wrap(chip + sign(r) * d)
        slot = n_far * r + d
        return remote((k_ref, v_ref)[h].at[seq(r, c)], kv.at[r, h, chip, core], KV, 2 * slot + h, 2 * slot + core, 2 * c + h)

    def relay(r, d, g):
        z = wrap(chip - sign(r) * d)
        t = 2 * (n_far * r + d) + g
        return remote(kv.at[r, core, z, g], kv.at[1 - r, core, z, g], RELAY, t, t, 2 * wrap(chip + sign(r)) + core)

    def share(r, z):
        return remote(kv.at[r, core, z], kv.at[r, core, z], SHARE, n_chip * r + z, n_chip * r + z, mate)

    def back(r, d, g, src, dst, kind):
        z = wrap(chip - sign(r) * d)
        slot = n_far * r + d
        return remote(src.at[slot, g], dst, kind, 2 * slot + g, 2 * slot + core, 2 * z + g)

    def part_copy(r):
        return remote(acc.at[r, 1 - core], part.at[r], PART, r, r, mate)

    def cross_copy(r, d):
        z = wrap(chip + sign(r) * (d + 1))
        i = 2 + n_far * r + d
        return remote(acc.at[r, core, z], cross.at[1 - r, d], PART, i, i, 2 * wrap(chip + sign(r)) + core)

    def own(r, h):
        slot = n_far * r
        b = seq(r, chip)
        return (pltpu.make_async_copy((k_ref, v_ref)[h].at[b], kv.at[r, h, chip, h], self_sem.at[KV, r]),
                pltpu.make_async_copy(q_ref.at[b, h], q_in.at[slot, h], self_sem.at[Q, r]),
                pltpu.make_async_copy(do_ref.at[b, h], do_in.at[slot, h], self_sem.at[DO, r]))

    def send_rows(d):
        for r in range(2):
            for h in range(2):
                out_q(r, d, h, q_ref, q_in, Q).start()
                out_q(r, d, h, do_ref, do_in, DO).start()

    for h in range(2):
        @pl.when(core == h)
        def _():
            for r in range(2):
                out_kv(r, 0, 1 - h).start()
                for cp in own(r, h):
                    cp.start()

    def send_kv(d, _):
        for r in range(2):
            for h in range(2):
                out_kv(r, d, h).start()
        return 0

    lax.fori_loop(1, n_far, send_kv, 0)

    for h in range(2):
        @pl.when(core == h)
        def _():
            for r in range(2):
                out_q(r, 0, 1 - h, q_ref, q_in, Q).start()
                out_q(r, 0, 1 - h, do_ref, do_in, DO).start()
            for r in range(2):
                for cp in own(r, h):
                    cp.wait()

    def pass_on(d, _):
        for r in range(2):
            for g in range(2):
                @pl.when(jnp.logical_or(d > 0, core != g))
                def _():
                    landed(kv.at[r, core, wrap(chip - sign(r) * d), g], KV, 2 * (n_far * r + d) + g).wait_recv()

                relay(r, d, g).start()
            share(r, wrap(chip - sign(r) * d)).start()
        return 0

    lax.fori_loop(0, n_far, pass_on, 0)

    def send_far(d, _):
        send_rows(d)
        return 0

    lax.fori_loop(1, n_far, send_far, 0)

    acc[...] = jnp.zeros(acc.shape, F32)

    def take(d, _):
        for r in range(2):
            z = wrap(chip + sign(r) * (d + 1))
            for g in range(2):
                landed(kv.at[r, core, z, g], RELAY, 2 * (n_far * (1 - r) + d) + g).wait_recv()
            share(r, z).start()
        return 0

    lax.fori_loop(0, n_far, take, 0)

    def turn(z, _):
        for r in range(2):
            landed(kv.at[r, 1 - core, z], SHARE, n_chip * r + z).wait_recv()
            kt[r, z] = kv[r, 0, z].reshape(keys, d_head).astype(F32).T.astype(BF16)
            vt[r, z] = kv[r, 1, z].reshape(keys, d_head).astype(F32).T.astype(BF16)
        return 0

    lax.fori_loop(0, n_chip, turn, 0)

    def add_part(r):
        part_copy(r).wait_recv()

        def add(z, _):
            acc[r, core, z] += part[r, z]
            return 0

        lax.fori_loop(0, n_chip, add, 0)

        def go(d, _):
            cross_copy(r, d).start()
            return 0

        lax.fori_loop(0, n_far, go, 0)

    def tile(n, _):
        r, d = lax.rem(n, 2), n // 2
        z = wrap(chip - sign(r) * d)
        slot = n_far * r + d

        @pl.when(n == 2 * n_far - 1)
        def _():
            part_copy(0).start()

        for g in range(2):
            @pl.when(jnp.logical_or(d > 0, core != g))
            def _():
                landed(q_in.at[slot, g], Q, 2 * slot + g).wait_recv()
                landed(do_in.at[slot, g], DO, 2 * slot + g).wait_recv()

        def q_rows():
            return q_in[slot].reshape(cols, d_head)

        def do_rows():
            return do_in[slot].reshape(cols, d_head)

        def block(kind, j):
            return kv[r, kind, j].reshape(keys, d_head)

        col = lax.broadcasted_iota(jnp.int32, (1, cols), 1)
        q_pos = col // (cols // 2) * (keys // 2) + core * (keys // 4) + lax.rem(col, cols // 2) // n_grp
        key_pos = lax.broadcasted_iota(jnp.int32, (keys, cols), 0)
        x = jnp.where(key_pos <= q_pos, dot_nt(block(0, z), q_rows()) * scale2, NEG_BIG)
        s_buf[z] = x
        m = jnp.max(x, axis=0, keepdims=True)
        p = jnp.exp2(x - m)
        l = jnp.sum(p, axis=0, keepdims=True)
        o_acc[...] = dot(vt[r, z], p.astype(BF16))

        def forward(j, carry):
            m, l = carry
            x = dot_nt(block(0, j), q_rows()) * scale2
            s_buf[j] = x
            m_new = jnp.maximum(m, jnp.max(x, axis=0, keepdims=True))
            a = jnp.exp2(m - m_new)
            p = jnp.exp2(x - m_new)
            l = l * a + jnp.sum(p, axis=0, keepdims=True)
            o_acc[...] = o_acc[...] * a + dot(vt[r, j], p.astype(BF16))
            return m_new, l

        m, l = lax.fori_loop(0, z, forward, (m, l))
        o_full = (o_acc[...] * (1.0 / l)).astype(BF16).astype(F32)
        o_st[slot] = o_full.T.astype(BF16).reshape(o_st.shape[1:])
        lse = m + jnp.log2(l)
        delta = jnp.sum(do_rows().astype(F32).T * o_full, axis=0, keepdims=True)
        dq_acc[...] = jnp.zeros(dq_acc.shape, F32)

        for g in range(2):
            @pl.when(jnp.logical_or(d > 0, core != g))
            def _():
                back(r, d, g, o_st, o_ref.at[seq(r, chip), core], O).start()

        def backward(j, _):
            p = jnp.exp2(s_buf[j] - lse)
            dp = dot_nt(block(1, j), do_rows())
            ds = (p * (dp - delta)).astype(BF16)
            acc[r, 1, j] += dot(p.astype(BF16), do_rows())
            acc[r, 0, j] += dot(ds, q_rows())
            dq_acc[...] += dot(kt[r, j], ds)
            return 0

        lax.fori_loop(0, z + 1, backward, 0)
        dq_st[slot] = (dq_acc[...] * scale).T.astype(BF16).reshape(dq_st.shape[1:])

        for g in range(2):
            @pl.when(jnp.logical_or(d > 0, core != g))
            def _():
                back(r, d, g, dq_st, dq_ref.at[seq(r, chip), core], DQ).start()

        return 0

    lax.fori_loop(0, 2 * n_far, tile, 0)
    part_copy(1).start()

    def own_out(r, h):
        slot, b = n_far * r, seq(r, chip)
        return (pltpu.make_async_copy(o_st.at[slot, h], o_ref.at[b, h], self_sem.at[O, r]),
                pltpu.make_async_copy(dq_st.at[slot, h], dq_ref.at[b, h], self_sem.at[DQ, r]),
                pltpu.make_async_copy(fin.at[slot, h], (dk_ref, dv_ref)[h].at[b], self_sem.at[FIN, r]))

    for h in range(2):
        @pl.when(core == h)
        def _():
            for r in range(2):
                own_out(r, h)[0].start()
                own_out(r, h)[1].start()

    add_part(0)
    add_part(1)

    factor = jnp.where(core == 0, scale, 1.0).astype(F32)

    for r in (1, 0):
        def finish(d, _):
            slot = n_far * r + d
            landed(cross.at[r, d], PART, 2 + n_far * (1 - r) + d).wait_recv()
            total = acc[r, core, wrap(chip - sign(r) * d)] + cross[r, d]
            fin[slot] = (total * factor).astype(BF16).reshape(fin.shape[1:])
            for h in range(2):
                for g in range(2):
                    @pl.when(jnp.logical_and(core == h, jnp.logical_or(d > 0, h != g)))
                    def _():
                        back(r, d, g, fin, (dk_ref, dv_ref)[h].at[seq(r, chip)], FIN).start()

            return 0

        lax.fori_loop(0, n_far, finish, 0)

    for h in range(2):
        @pl.when(core == h)
        def _():
            for r in range(2):
                own_out(r, h)[2].start()

    def drain(d, _):
        for r in range(2):
            slot = n_far * r + d
            c = wrap(chip + sign(r) * d)
            cross_copy(r, d).wait_send()
            share(r, d).wait_send()
            share(r, d + n_far).wait_send()
            for h in range(2):
                t = 2 * slot + h
                relay(r, d, h).wait_send()

                @pl.when(jnp.logical_or(d > 0, core != h))
                def _():
                    landed(q_in.at[slot, h], Q, t).wait_send()
                    landed(do_in.at[slot, h], DO, t).wait_send()
                    landed(kv.at[r, 0, d, h], KV, t).wait_send()
                    landed(o_st.at[slot, h], O, t).wait_send()
                    landed(dq_st.at[slot, h], DQ, t).wait_send()
                    landed(fin.at[slot, h], FIN, t).wait_send()
                    landed(o_ref.at[seq(r, c), h], O, t).wait_recv()
                    landed(dq_ref.at[seq(r, c), h], DQ, t).wait_recv()
                    landed((dk_ref, dv_ref)[h].at[seq(r, c)], FIN, t).wait_recv()

        return 0

    lax.fori_loop(0, n_far, drain, 0)
    for r in range(2):
        part_copy(r).wait_send()
    for h in range(2):
        @pl.when(core == h)
        def _():
            for r in range(2):
                for cp in own_out(r, h):
                    cp.wait()


def solution(mesh):
    part_spec = P("dp", "ctx")
    n_ctx = mesh.shape["ctx"]
    n_chip = n_ctx // 2
    n_far = n_chip // 2

    def local_step(queries, keys, values, grad_out):
        n_batch, c_len, n_q, d_head = queries.shape
        assert keys.shape[2] == 1 and n_batch == n_chip
        rows = c_len * n_q // 2
        q_shape = (n_batch, 2, rows, d_head)
        kv_shape = (n_batch, c_len, d_head)
        hbm = pl.BlockSpec(memory_space=pl.ANY)
        vmem = pltpu.VMEM
        tiles = vmem((2 * n_far, 2, rows, d_head), BF16)
        out, grad_q, grad_k, grad_v = pl.pallas_call(
            functools.partial(kernel, n_chip, n_q, d_head ** -0.5),
            out_shape=tuple(jax.ShapeDtypeStruct(s, BF16) for s in (q_shape, q_shape, kv_shape, kv_shape)),
            in_specs=[hbm] * 4,
            out_specs=(hbm,) * 4,
            scratch_shapes=[
                tiles,
                tiles,
                vmem((2, 2, n_chip, 2, c_len, d_head), BF16),
                vmem((2, n_chip, d_head, 2 * c_len), BF16),
                vmem((2, n_chip, d_head, 2 * c_len), BF16),
                vmem((2, 2, n_chip, 2 * c_len, d_head), F32),
                vmem((2, n_chip, 2 * c_len, d_head), F32),
                vmem((2, n_far, 2 * c_len, d_head), F32),
                tiles,
                tiles,
                vmem((2 * n_far, 2, c_len, d_head), BF16),
                vmem((n_chip, 2 * c_len, 2 * rows), F32),
                vmem((d_head, 2 * rows), F32),
                vmem((d_head, 2 * rows), F32),
                pltpu.SemaphoreType.DMA((N_KIND, n_ctx)),
                pltpu.SemaphoreType.DMA((N_KIND, n_ctx)),
                pltpu.SemaphoreType.DMA((N_KIND, 2)),
            ],
            compiler_params=pltpu.CompilerParams(collective_id=0, has_side_effects=True, vmem_limit_bytes=62 * 2 ** 20),
        )(queries.reshape(q_shape), grad_out.reshape(q_shape), keys.reshape(kv_shape), values.reshape(kv_shape))
        return (out.reshape(queries.shape), grad_q.reshape(queries.shape), grad_k.reshape(keys.shape), grad_v.reshape(values.shape))

    return jax.shard_map(local_step, mesh=mesh, in_specs=(part_spec,) * 4, out_specs=(part_spec,) * 4, check_vma=False)
```

time: 781 us -> 230 us (0.29)
  waiting for transfers between devices: 632 us -> 0 us
  Pallas kernels: 0 us -> 222 us
  other arithmetic: 42.5 us -> 0 us
  local copies, waits for them, and re-layouts: 48.6 us -> 6.74 us
  matrix products: 41.4 us -> 0 us
  between operations: 13.8 us -> 0.65 us
    reduce_scatter x2 -> x0, waiting for transfers between devices: 531 us -> none  [the longest x1 435 us: local_step(): dv_sum = lax.psum_scatter(dv_all, 'ctx', scatter_dimension=1)]
    pallas_call x0 -> x1, Pallas kernels: none -> 222 us  [local_step(): pl.pallas_call(functools.partial(kernel, n_chip, n_q, d_head ** (-0.5)),...]
    all_gather x2 -> x0, waiting for transfers between devices: 98.8 us -> none  [the longest x1 53.7 us: local_step(): k_all = lax.all_gather(keys, 'ctx', axis=1)]
    dot_general x14 -> x0, matrix products: 41.4 us -> none  [the longest x4 9.97 us: block_scores(): jnp.einsum('bihgd,bjhd->bhgij', q_heads, k_blk, preferred_element_type=jn...]
    unnamed x1 -> x0, other arithmetic: 31.2 us -> none
    broadcast_in_dim x6 -> x0, local copies, waits for them, and re-layouts: 20.7 us -> none  [the longest x2 15.7 us: attend_backward(): acc_zero = jnp.zeros(k_all.shape, jnp.float32)]
    while x24 -> x0, local copies, waits for them, and re-layouts: 19.2 us -> none  [the longest x2 15.4 us: attend_forward(): m_fin, l_fin, acc_fin = lax.fori_loop(0, dev_idx + 1, loop_body, init_carry)]
  transfers between devices with their start and end apart: 4 -> 0, of which waited for: 4 -> 0; matrix products, arithmetic and copies ran while one was open for 3% -> 0% of each run, Pallas kernels for 0% -> 0%
where the time goes in v2:
time: 230 us
  Pallas kernels  222 us (97%)
  local copies, waits for them, and re-layouts  6.74 us (3%)
    pallas_call x1, Pallas kernels, local_step(): pl.pallas_call(functools.partial(kernel, n_chip, n_q, d_head ** (-0.5)),...  222 us
    unnamed x10, local copies, waits for them, and re-layouts  6.74 us

profile of v2, /device:TPU:21, one launch (start us, length us, event | category | flops | bytes accessed | tf_op | source)
XLA Modules:
  0.0 229.5 jit_solution(2580832939270071862)
XLA Ops:
  0.6 222.1 %shard_map.75 = (bf16[8,2,512,128]{3,2,1,0:T(8,128)(2,1)}, bf16[8,2,512,128]{3,2,1,0:T(8,128)(2,1)}, bf16[8,256,128]{2,1,0:T(8,128)(2,1)}, bf16[8,256,128]{2,1,0:T(8,128)(2,1)}) custom-call(bf16[8,2,512,128]{3,2,1,0:T(8,128)(2,1)} %bitcast.12, bf16[8,2,512,128]{3,2,1,0:T(8,128)(2,1)} %bitcast.13, bf16[8,256,128]{2,1,0:T(8,128)(2,1)} %bitcast.16, ...), custom_call_target="tpu_custom_call" | custom-call | tf_op jit(solution)/shard_map/pallas_call | solution.py:359
  222.8 0.0 copy-start
  222.8 3.8 %copy.14 = bf16[8,256,4,128]{3,2,1,0:T(4,128)(2,1)} copy(bf16[8,256,4,128]{3,2,1,0:T(4,128)(2,1)} %bitcast.15) | data formatting | bytes 4194304
  226.6 0.0 copy-done
  226.6 0.0 copy-start.2
  226.6 0.0 copy-start.1
  226.6 1.3 copy.15
  227.9 0.1 copy-done.2
  228.0 0.8 copy.16
  228.7 0.0 copy-done.1
  228.8 0.8 copy.17
Async XLA Ops:
  222.8 3.8 %copy-start = (bf16[8,2,512,128]{3,2,1,0:T(8,128)(2,1)S(1)}, bf16[8,2,512,128]{3,2,1,0:T(8,128)(2,1)}, u32[]{:S(2)}) copy-start(bf16[8,2,512,128]{3,2,1,0:T(8,128)(2,1)} %get-tuple-element.9) | copy-start | bytes 6291460
  226.6 1.4 copy-start.2
  226.6 2.2 copy-start.1

commit v3 on v2

--- a/solution.py
+++ b/solution.py
@@ -27,7 +27,6 @@
 def kernel(n_chip, n_grp, scale, q_ref, do_ref, k_ref, v_ref, o_ref, dq_ref, dk_ref, dv_ref,
            q_in, do_in, kv, kt, vt, acc, part, cross, o_st, dq_st, fin, s_buf, o_acc, dq_acc,
            send, recv, self_sem):
-    n_dev = 2 * n_chip
     n_far = n_chip // 2
     me = lax.axis_index("ctx")
     chip, core = me // 2, me % 2
@@ -38,21 +37,33 @@
 
     barrier = pltpu.get_barrier_semaphore()
 
-    def greet(s, _):
-        pl.semaphore_signal(barrier, inc=1, device_id={"ctx": lax.rem(me + s, n_dev)}, device_id_type=MESH)
-        return 0
-
-    lax.fori_loop(1, n_dev, greet, 0)
-    pl.semaphore_wait(barrier, n_dev - 1)
-
     def wrap(c):
         return lax.rem(c + 2 * n_chip, n_chip)
 
+    pl.semaphore_signal(barrier, inc=1, device_id={"ctx": mate}, device_id_type=MESH)
+
+    def greet(d, _):
+        for c in (wrap(chip + d), wrap(chip - d)):
+            for h in range(2):
+                pl.semaphore_signal(barrier, inc=1, device_id={"ctx": 2 * c + h}, device_id_type=MESH)
+        return 0
+
+    lax.fori_loop(1, n_far, greet, 0)
+    pl.semaphore_wait(barrier, 4 * n_far - 3)
+
     def sign(r):
         return 1 - 2 * r
 
     def seq(r, c):
         return wrap(c - r)
+
+    def last(r, c):
+        if r == 0:
+            return jnp.where(c >= n_far - 1, c, n_chip - 1)
+        return jnp.where(c <= n_chip - n_far, c + n_far - 1, n_chip - 1)
+
+    def reads(r, c, z):
+        return z <= last(r, c)
 
     def remote(src, dst, kind, s_idx, r_idx, dev):
         return pltpu.make_async_remote_copy(src_ref=src, dst_ref=dst, send_sem=send.at[kind, s_idx], recv_sem=recv.at[kind, r_idx],
@@ -75,6 +86,9 @@
         z = wrap(chip - sign(r) * d)
         t = 2 * (n_far * r + d) + g
         return remote(kv.at[r, core, z, g], kv.at[1 - r, core, z, g], RELAY, t, t, 2 * wrap(chip + sign(r)) + core)
+
+    def relayed(r, d):
+        return reads(1 - r, wrap(chip + sign(r)), wrap(chip - sign(r) * d))
 
     def share(r, z):
         return remote(kv.at[r, core, z], kv.at[r, core, z], SHARE, n_chip * r + z, n_chip * r + z, mate)
@@ -113,7 +127,8 @@
                 for cp in own(r, h):
                     cp.start()
 
-    def send_kv(d, _):
+    def send_kv(n, _):
+        d = n_far - n
         for r in range(2):
             for h in range(2):
                 out_kv(r, d, h).start()
@@ -138,7 +153,9 @@
                 def _():
                     landed(kv.at[r, core, wrap(chip - sign(r) * d), g], KV, 2 * (n_far * r + d) + g).wait_recv()
 
-                relay(r, d, g).start()
+                @pl.when(relayed(r, d))
+                def _():
+                    relay(r, d, g).start()
             share(r, wrap(chip - sign(r) * d)).start()
         return 0
 
@@ -155,18 +172,25 @@
     def take(d, _):
         for r in range(2):
             z = wrap(chip + sign(r) * (d + 1))
-            for g in range(2):
-                landed(kv.at[r, core, z, g], RELAY, 2 * (n_far * (1 - r) + d) + g).wait_recv()
-            share(r, z).start()
+
+            @pl.when(reads(r, chip, z))
+            def _():
+                for g in range(2):
+                    landed(kv.at[r, core, z, g], RELAY, 2 * (n_far * (1 - r) + d) + g).wait_recv()
+                share(r, z).start()
+
         return 0
 
     lax.fori_loop(0, n_far, take, 0)
 
     def turn(z, _):
         for r in range(2):
-            landed(kv.at[r, 1 - core, z], SHARE, n_chip * r + z).wait_recv()
-            kt[r, z] = kv[r, 0, z].reshape(keys, d_head).astype(F32).T.astype(BF16)
-            vt[r, z] = kv[r, 1, z].reshape(keys, d_head).astype(F32).T.astype(BF16)
+            @pl.when(reads(r, chip, z))
+            def _():
+                landed(kv.at[r, 1 - core, z], SHARE, n_chip * r + z).wait_recv()
+                kt[r, z] = kv[r, 0, z].reshape(keys, d_head).astype(F32).T.astype(BF16)
+                vt[r, z] = kv[r, 1, z].reshape(keys, d_head).astype(F32).T.astype(BF16)
+
         return 0
 
     lax.fori_loop(0, n_chip, turn, 0)
@@ -180,8 +204,13 @@
 
         lax.fori_loop(0, n_chip, add, 0)
 
-        def go(d, _):
-            cross_copy(r, d).start()
+        def go(n, _):
+            d = n_far - 1 - n
+
+            @pl.when(reads(r, chip, wrap(chip + sign(r) * (d + 1))))
+            def _():
+                cross_copy(r, d).start()
+
             return 0
 
         lax.fori_loop(0, n_far, go, 0)
@@ -283,21 +312,26 @@
 
     factor = jnp.where(core == 0, scale, 1.0).astype(F32)
 
-    for r in (1, 0):
-        def finish(d, _):
+    def finish(n, _):
+        d = n_far - 1 - n
+        for r in range(2):
             slot = n_far * r + d
-            landed(cross.at[r, d], PART, 2 + n_far * (1 - r) + d).wait_recv()
-            total = acc[r, core, wrap(chip - sign(r) * d)] + cross[r, d]
-            fin[slot] = (total * factor).astype(BF16).reshape(fin.shape[1:])
+            z = wrap(chip - sign(r) * d)
+
+            @pl.when(relayed(r, d))
+            def _():
+                landed(cross.at[r, d], PART, 2 + n_far * (1 - r) + d).wait_recv()
+                acc[r, core, z] += cross[r, d]
+
+            fin[slot] = (acc[r, core, z] * factor).astype(BF16).reshape(fin.shape[1:])
             for h in range(2):
                 for g in range(2):
                     @pl.when(jnp.logical_and(core == h, jnp.logical_or(d > 0, h != g)))
                     def _():
                         back(r, d, g, fin, (dk_ref, dv_ref)[h].at[seq(r, chip)], FIN).start()
-
-            return 0
-
-        lax.fori_loop(0, n_far, finish, 0)
+        return 0
+
+    lax.fori_loop(0, n_far, finish, 0)
 
     for h in range(2):
         @pl.when(core == h)
@@ -309,12 +343,21 @@
         for r in range(2):
             slot = n_far * r + d
             c = wrap(chip + sign(r) * d)
-            cross_copy(r, d).wait_send()
-            share(r, d).wait_send()
-            share(r, d + n_far).wait_send()
+            for z in (d, d + n_far):
+                @pl.when(reads(r, chip, z))
+                def _():
+                    share(r, z).wait_send()
+
+            @pl.when(reads(r, chip, wrap(chip + sign(r) * (d + 1))))
+            def _():
+                cross_copy(r, d).wait_send()
+
             for h in range(2):
                 t = 2 * slot + h
-                relay(r, d, h).wait_send()
+
+                @pl.when(relayed(r, d))
+                def _():
+                    relay(r, d, h).wait_send()
 
                 @pl.when(jnp.logical_or(d > 0, core != h))
                 def _():
@@ -339,6 +382,34 @@
             for r in range(2):
                 for cp in own_out(r, h):
                     cp.wait()
+
+
+def copy_kernel(*refs):
+    n = (len(refs) - 2) // 3
+    src, dst, buf, sem_in, sem_out = refs[:n], refs[n:2 * n], refs[2 * n:3 * n], refs[-2], refs[-1]
+    pieces = [(a, b) for a in range(n) for b in range(src[a].shape[0])]
+    ins = [pltpu.make_async_copy(src[a].at[b], buf[a].at[b], sem_in.at[a, b]) for a, b in pieces]
+    outs = [pltpu.make_async_copy(buf[a].at[b], dst[a].at[b], sem_out.at[a, b]) for a, b in pieces]
+    for cp in ins:
+        cp.start()
+    for cp_in, cp_out in zip(ins, outs):
+        cp_in.wait()
+        cp_out.start()
+    for cp in outs:
+        cp.wait()
+
+
+def settle(*arrays):
+    hbm = pl.BlockSpec(memory_space=pl.ANY)
+    n = len(arrays)
+    sems = pltpu.SemaphoreType.DMA((n, arrays[0].shape[0]))
+    return pl.pallas_call(
+        copy_kernel,
+        out_shape=tuple(jax.ShapeDtypeStruct(a.shape, a.dtype) for a in arrays),
+        in_specs=[hbm] * n,
+        out_specs=(hbm,) * n,
+        scratch_shapes=[pltpu.VMEM(a.shape, a.dtype) for a in arrays] + [sems, sems],
+    )(*arrays)
 
 
 def solution(mesh):
@@ -382,6 +453,7 @@
             ],
             compiler_params=pltpu.CompilerParams(collective_id=0, has_side_effects=True, vmem_limit_bytes=62 * 2 ** 20),
         )(queries.reshape(q_shape), grad_out.reshape(q_shape), keys.reshape(kv_shape), values.reshape(kv_shape))
+        out, grad_q, grad_k, grad_v = settle(out, grad_q, grad_k, grad_v)
         return (out.reshape(queries.shape), grad_q.reshape(queries.shape), grad_k.reshape(keys.shape), grad_v.reshape(values.shape))
 
     return jax.shard_map(local_step, mesh=mesh, in_specs=(part_spec,) * 4, out_specs=(part_spec,) * 4, check_vma=False)

time: 230 us -> 221 us (0.961)
  local copies, waits for them, and re-layouts: 6.74 us -> 0 us
    pallas_call x1, Pallas kernels: 222 us -> 215 us  [local_step(): pl.pallas_call(functools.partial(kernel, n_chip, n_q, d_head ** (-0.5)),...]
    unnamed x10 -> x0, local copies, waits for them, and re-layouts: 6.74 us -> none
    pallas_call x0 -> x1, Pallas kernels: none -> 5.08 us  [settle(): pl.pallas_call(copy_kernel, out_shape=tuple((jax.ShapeDtypeStruct(a.shape...]
where the time goes in v3:
time: 221 us
  Pallas kernels  220 us (100%)
    pallas_call x1, Pallas kernels, local_step(): pl.pallas_call(functools.partial(kernel, n_chip, n_q, d_head ** (-0.5)),...  215 us
    pallas_call x1, Pallas kernels, settle(): pl.pallas_call(copy_kernel, out_shape=tuple((jax.ShapeDtypeStruct(a.shape...  5.08 us

profile of v3, /device:TPU:21, one launch (start us, length us, event | category | flops | bytes accessed | tf_op | source)
XLA Modules:
  0.0 221.1 jit_solution(617414949729808922)
XLA Ops:
  0.6 215.3 %shard_map.75 = (bf16[8,2,512,128]{3,2,1,0:T(8,128)(2,1)}, bf16[8,2,512,128]{3,2,1,0:T(8,128)(2,1)}, bf16[8,256,128]{2,1,0:T(8,128)(2,1)}, bf16[8,256,128]{2,1,0:T(8,128)(2,1)}) custom-call(bf16[8,2,512,128]{3,2,1,0:T(8,128)(2,1)} %bitcast.12, bf16[8,2,512,128]{3,2,1,0:T(8,128)(2,1)} %bitcast.13, bf16[8,256,128]{2,1,0:T(8,128)(2,1)} %bitcast.14, ...), custom_call_target="tpu_custom_call" | custom-call | tf_op jit(solution)/shard_map/pallas_call | solution.py:430
  216.0 5.1 %shard_map.76 = (bf16[8,2,512,128]{3,2,1,0:T(8,128)(2,1)}, bf16[8,2,512,128]{3,2,1,0:T(8,128)(2,1)}, bf16[8,256,128]{2,1,0:T(8,128)(2,1)}, bf16[8,256,128]{2,1,0:T(8,128)(2,1)}) custom-call(bf16[8,2,512,128]{3,2,1,0:T(8,128)(2,1)} %get-tuple-element.12.refs_0_, bf16[8,2,512,128]{3,2,1,0:T(8,128)(2,1)} %get-tuple-element.13.refs_1_, ...), custom_call_target="tpu_custom_call" | custom-call | tf_op jit(solution)/shard_map/pallas_call | solution.py:406

commit v4 on v3

--- a/solution.py
+++ b/solution.py
@@ -13,7 +13,8 @@
 NT = (((1,), (1,)), ((), ()))
 F32 = jnp.float32
 BF16 = jnp.bfloat16
-Q, DO, KV, RELAY, SHARE, O, DQ, FIN, PART, N_KIND = range(10)
+Q, DO, KV, RELAY, SHARE, O, DQ, FIN, PART, HOME, N_KIND = range(11)
+H_Q, H_DO, H_K, H_V, H_O, H_DQ, H_FIN, H_PART = range(0, 16, 2)
 
 
 def dot(a, b):
@@ -26,7 +27,8 @@
 
 def kernel(n_chip, n_grp, scale, q_ref, do_ref, k_ref, v_ref, o_ref, dq_ref, dk_ref, dv_ref,
            q_in, do_in, kv, kt, vt, acc, part, cross, o_st, dq_st, fin, s_buf, o_acc, dq_acc,
-           send, recv, self_sem):
+           h_q, h_do, h_kv, h_o, h_dq, h_acc, h_part, h_cross, h_fin,
+           send, recv, self_sem, home_sem):
     n_far = n_chip // 2
     me = lax.axis_index("ctx")
     chip, core = me // 2, me % 2
@@ -87,6 +89,12 @@
         t = 2 * (n_far * r + d) + g
         return remote(kv.at[r, core, z, g], kv.at[1 - r, core, z, g], RELAY, t, t, 2 * wrap(chip + sign(r)) + core)
 
+    def stays(d, z):
+        return jnp.logical_and(d == n_far - 1, z == 0)
+
+    def leaves(d, z):
+        return jnp.logical_or(d < n_far - 1, z > 0)
+
     def relayed(r, d):
         return reads(1 - r, wrap(chip + sign(r)), wrap(chip - sign(r) * d))
 
@@ -162,10 +170,78 @@
     lax.fori_loop(0, n_far, pass_on, 0)
 
     def send_far(d, _):
-        send_rows(d)
+        @pl.when(leaves(d, chip))
+        def _():
+            send_rows(d)
+
         return 0
 
     lax.fori_loop(1, n_far, send_far, 0)
+
+    def diagonal(k_rows, q_rows):
+        col = lax.broadcasted_iota(jnp.int32, (1, cols), 1)
+        q_pos = col // (cols // 2) * (keys // 2) + core * (keys // 4) + lax.rem(col, cols // 2) // n_grp
+        key_pos = lax.broadcasted_iota(jnp.int32, (keys, cols), 0)
+        return jnp.where(key_pos <= q_pos, dot_nt(k_rows, q_rows) * scale2, NEG_BIG)
+
+    def to_mate(src, dst, i):
+        return remote(src, dst, HOME, i, i, mate)
+
+    def stay(src, dst, i):
+        return pltpu.make_async_copy(src, dst, home_sem.at[i])
+
+    def home_in(t, move, half):
+        b = n_far - 1 + t
+        return (move(q_ref.at[b, half], h_q.at[t, core], H_Q + t), move(do_ref.at[b, half], h_do.at[t, core], H_DO + t),
+                move(k_ref.at[b], h_kv.at[t, 0, core], H_K + t), move(v_ref.at[b], h_kv.at[t, 1, core], H_V + t))
+
+    def home_out(t, move, half):
+        b = n_far - 1 + t
+        return (move(h_o.at[t, half], o_ref.at[b, core], H_O + t), move(h_dq.at[t, half], dq_ref.at[b, core], H_DQ + t))
+
+    def home_part(t):
+        return to_mate(h_acc.at[t, 1 - core], h_part.at[t], H_PART + t)
+
+    def home_fin(t, h):
+        out = (dk_ref, dv_ref)[h].at[n_far - 1 + t]
+        return stay(h_fin.at[t, h], out, H_FIN + t), to_mate(h_fin.at[t, 1 - h], out, H_FIN + t)
+
+    @pl.when(chip == 0)
+    def _():
+        for t in range(2):
+            for cp in home_in(t, to_mate, 1 - core) + home_in(t, stay, core):
+                cp.start()
+        for t in range(2):
+            for cp in home_in(t, stay, core):
+                cp.wait()
+            for cp in home_in(t, to_mate, 1 - core):
+                cp.wait()
+
+        def home_tile(t, _):
+            q_rows, do_rows = h_q[t].reshape(cols, d_head), h_do[t].reshape(cols, d_head)
+            k_rows, v_rows = h_kv[t, 0].reshape(keys, d_head), h_kv[t, 1].reshape(keys, d_head)
+            x = diagonal(k_rows, q_rows)
+            s_buf[0] = x
+            m = jnp.max(x, axis=0, keepdims=True)
+            p = jnp.exp2(x - m)
+            l = jnp.sum(p, axis=0, keepdims=True)
+            o = dot(v_rows.astype(F32).T.astype(BF16), p.astype(BF16))
+            o_full = (o * (1.0 / l)).astype(BF16).astype(F32)
+            h_o[t] = o_full.T.astype(BF16).reshape(h_o.shape[1:])
+            delta = jnp.sum(do_rows.astype(F32).T * o_full, axis=0, keepdims=True)
+            p = jnp.exp2(s_buf[0] - (m + jnp.log2(l)))
+            ds = (p * (dot_nt(v_rows, do_rows) - delta)).astype(BF16)
+            h_acc[t, 1] = dot(p.astype(BF16), do_rows)
+            h_acc[t, 0] = dot(ds, q_rows)
+            dq = dot(k_rows.astype(F32).T.astype(BF16), ds)
+            h_dq[t] = (dq * scale).T.astype(BF16).reshape(h_dq.shape[1:])
+            return 0
+
+        lax.fori_loop(0, 2, home_tile, 0)
+        for t in range(2):
+            for cp in home_out(t, to_mate, 1 - core) + home_out(t, stay, core):
+                cp.start()
+            home_part(t).start()
 
     acc[...] = jnp.zeros(acc.shape, F32)
 
@@ -224,6 +300,14 @@
         def _():
             part_copy(0).start()
 
+        @pl.when(leaves(d, z))
+        def _():
+            work(r, d, z, slot)
+
+        return 0
+
+    def work(r, d, z, slot):
+
         for g in range(2):
             @pl.when(jnp.logical_or(d > 0, core != g))
             def _():
@@ -239,10 +323,7 @@
         def block(kind, j):
             return kv[r, kind, j].reshape(keys, d_head)
 
-        col = lax.broadcasted_iota(jnp.int32, (1, cols), 1)
-        q_pos = col // (cols // 2) * (keys // 2) + core * (keys // 4) + lax.rem(col, cols // 2) // n_grp
-        key_pos = lax.broadcasted_iota(jnp.int32, (keys, cols), 0)
-        x = jnp.where(key_pos <= q_pos, dot_nt(block(0, z), q_rows()) * scale2, NEG_BIG)
+        x = diagonal(block(0, z), q_rows())
         s_buf[z] = x
         m = jnp.max(x, axis=0, keepdims=True)
         p = jnp.exp2(x - m)
@@ -289,8 +370,6 @@
             def _():
                 back(r, d, g, dq_st, dq_ref.at[seq(r, chip), core], DQ).start()
 
-        return 0
-
     lax.fori_loop(0, 2 * n_far, tile, 0)
     part_copy(1).start()
 
@@ -312,6 +391,9 @@
 
     factor = jnp.where(core == 0, scale, 1.0).astype(F32)
 
+    def home_cross(r):
+        return remote(acc.at[r, core, 0], h_cross.at[r], PART, 2 + 2 * n_far + r, 2 + 2 * n_far + r, core)
+
     def finish(n, _):
         d = n_far - 1 - n
         for r in range(2):
@@ -326,9 +408,14 @@
             fin[slot] = (acc[r, core, z] * factor).astype(BF16).reshape(fin.shape[1:])
             for h in range(2):
                 for g in range(2):
-                    @pl.when(jnp.logical_and(core == h, jnp.logical_or(d > 0, h != g)))
+                    @pl.when(jnp.logical_and(leaves(d, z), jnp.logical_and(core == h, jnp.logical_or(d > 0, h != g))))
                     def _():
                         back(r, d, g, fin, (dk_ref, dv_ref)[h].at[seq(r, chip)], FIN).start()
+
+            @pl.when(stays(d, z))
+            def _():
+                home_cross(r).start()
+
         return 0
 
     lax.fori_loop(0, n_far, finish, 0)
@@ -338,6 +425,28 @@
         def _():
             for r in range(2):
                 own_out(r, h)[2].start()
+
+    @pl.when(chip == 0)
+    def _():
+        for t in range(2):
+            home_part(t).wait()
+            landed(h_cross.at[t], PART, 2 + 2 * n_far + t).wait_recv()
+            total = h_acc[t, core] + h_part[t] + h_cross[t]
+            h_fin[t] = (total * factor).astype(BF16).reshape(h_fin.shape[1:])
+        for h in range(2):
+            @pl.when(core == h)
+            def _():
+                for t in range(2):
+                    for cp in home_fin(t, h):
+                        cp.start()
+                for t in range(2):
+                    kept, sent = home_fin(t, h)
+                    kept.wait()
+                    sent.wait_send()
+                    landed((dk_ref, dv_ref)[1 - h].at[n_far - 1 + t], HOME, H_FIN + t).wait_recv()
+        for t in range(2):
+            for cp in home_out(t, to_mate, 1 - core) + home_out(t, stay, core):
+                cp.wait()
 
     def drain(d, _):
         for r in range(2):
@@ -359,17 +468,29 @@
                 def _():
                     relay(r, d, h).wait_send()
 
-                @pl.when(jnp.logical_or(d > 0, core != h))
+                away = jnp.logical_or(d > 0, core != h)
+
+                @pl.when(away)
+                def _():
+                    landed(kv.at[r, 0, d, h], KV, t).wait_send()
+
+                @pl.when(jnp.logical_and(away, leaves(d, chip)))
                 def _():
                     landed(q_in.at[slot, h], Q, t).wait_send()
                     landed(do_in.at[slot, h], DO, t).wait_send()
-                    landed(kv.at[r, 0, d, h], KV, t).wait_send()
+                    landed(o_ref.at[seq(r, c), h], O, t).wait_recv()
+                    landed(dq_ref.at[seq(r, c), h], DQ, t).wait_recv()
+                    landed((dk_ref, dv_ref)[h].at[seq(r, c)], FIN, t).wait_recv()
+
+                @pl.when(jnp.logical_and(away, leaves(d, wrap(chip - sign(r) * d))))
+                def _():
                     landed(o_st.at[slot, h], O, t).wait_send()
                     landed(dq_st.at[slot, h], DQ, t).wait_send()
                     landed(fin.at[slot, h], FIN, t).wait_send()
-                    landed(o_ref.at[seq(r, c), h], O, t).wait_recv()
-                    landed(dq_ref.at[seq(r, c), h], DQ, t).wait_recv()
-                    landed((dk_ref, dv_ref)[h].at[seq(r, c)], FIN, t).wait_recv()
+
+            @pl.when(stays(d, wrap(chip - sign(r) * d)))
+            def _():
+                home_cross(r).wait_send()
 
         return 0
 
@@ -447,9 +568,19 @@
                 vmem((n_chip, 2 * c_len, 2 * rows), F32),
                 vmem((d_head, 2 * rows), F32),
                 vmem((d_head, 2 * rows), F32),
+                vmem((2, 2, rows, d_head), BF16),
+                vmem((2, 2, rows, d_head), BF16),
+                vmem((2, 2, 2, c_len, d_head), BF16),
+                vmem((2, 2, rows, d_head), BF16),
+                vmem((2, 2, rows, d_head), BF16),
+                vmem((2, 2, 2 * c_len, d_head), F32),
+                vmem((2, 2 * c_len, d_head), F32),
+                vmem((2, 2 * c_len, d_head), F32),
+                vmem((2, 2, c_len, d_head), BF16),
                 pltpu.SemaphoreType.DMA((N_KIND, n_ctx)),
                 pltpu.SemaphoreType.DMA((N_KIND, n_ctx)),
                 pltpu.SemaphoreType.DMA((N_KIND, 2)),
+                pltpu.SemaphoreType.DMA((16,)),
             ],
             compiler_params=pltpu.CompilerParams(collective_id=0, has_side_effects=True, vmem_limit_bytes=62 * 2 ** 20),
         )(queries.reshape(q_shape), grad_out.reshape(q_shape), keys.reshape(kv_shape), values.reshape(kv_shape))

time: 221 us -> 216 us (0.977)
  Pallas kernels: 220 us -> 214 us
    pallas_call x1, Pallas kernels: 215 us -> 209 us  [local_step(): pl.pallas_call(functools.partial(kernel, n_chip, n_q, d_head ** (-0.5)),...]
where the time goes in v4:
time: 216 us; the launch traced here: 215 us
  Pallas kernels  214 us (99%)
    pallas_call x1, Pallas kernels, local_step(): pl.pallas_call(functools.partial(kernel, n_chip, n_q, d_head ** (-0.5)),...  209 us
    pallas_call x1, Pallas kernels, settle(): pl.pallas_call(copy_kernel, out_shape=tuple((jax.ShapeDtypeStruct(a.shape...  5.08 us

profile of v4, /device:TPU:21, one launch (start us, length us, event | category | flops | bytes accessed | tf_op | source)
XLA Modules:
  0.0 214.7 jit_solution(12585613565951773673)
XLA Ops:
  0.6 208.9 %shard_map.75 = (bf16[8,2,512,128]{3,2,1,0:T(8,128)(2,1)}, bf16[8,2,512,128]{3,2,1,0:T(8,128)(2,1)}, bf16[8,256,128]{2,1,0:T(8,128)(2,1)}, bf16[8,256,128]{2,1,0:T(8,128)(2,1)}) custom-call(bf16[8,2,512,128]{3,2,1,0:T(8,128)(2,1)} %bitcast.12, bf16[8,2,512,128]{3,2,1,0:T(8,128)(2,1)} %bitcast.13, bf16[8,256,128]{2,1,0:T(8,128)(2,1)} %bitcast.14, ...), custom_call_target="tpu_custom_call" | custom-call | tf_op jit(solution)/shard_map/pallas_call | solution.py:551
  209.6 5.1 %shard_map.76 = (bf16[8,2,512,128]{3,2,1,0:T(8,128)(2,1)}, bf16[8,2,512,128]{3,2,1,0:T(8,128)(2,1)}, bf16[8,256,128]{2,1,0:T(8,128)(2,1)}, bf16[8,256,128]{2,1,0:T(8,128)(2,1)}) custom-call(bf16[8,2,512,128]{3,2,1,0:T(8,128)(2,1)} %get-tuple-element.12.refs_0_, bf16[8,2,512,128]{3,2,1,0:T(8,128)(2,1)} %get-tuple-element.13.refs_1_, ...), custom_call_target="tpu_custom_call" | custom-call | tf_op jit(solution)/shard_map/pallas_call | solution.py:527

commit v5 on v4

--- a/solution.py
+++ b/solution.py
@@ -44,7 +44,8 @@
 
     pl.semaphore_signal(barrier, inc=1, device_id={"ctx": mate}, device_id_type=MESH)
 
-    def greet(d, _):
+    def greet(n, _):
+        d = n_far - n
         for c in (wrap(chip + d), wrap(chip - d)):
             for h in range(2):
                 pl.semaphore_signal(barrier, inc=1, device_id={"ctx": 2 * c + h}, device_id_type=MESH)
@@ -508,9 +509,8 @@
 def copy_kernel(*refs):
     n = (len(refs) - 2) // 3
     src, dst, buf, sem_in, sem_out = refs[:n], refs[n:2 * n], refs[2 * n:3 * n], refs[-2], refs[-1]
-    pieces = [(a, b) for a in range(n) for b in range(src[a].shape[0])]
-    ins = [pltpu.make_async_copy(src[a].at[b], buf[a].at[b], sem_in.at[a, b]) for a, b in pieces]
-    outs = [pltpu.make_async_copy(buf[a].at[b], dst[a].at[b], sem_out.at[a, b]) for a, b in pieces]
+    ins = [pltpu.make_async_copy(src[a], buf[a], sem_in.at[a]) for a in range(n)]
+    outs = [pltpu.make_async_copy(buf[a], dst[a], sem_out.at[a]) for a in range(n)]
     for cp in ins:
         cp.start()
     for cp_in, cp_out in zip(ins, outs):
@@ -523,7 +523,7 @@
 def settle(*arrays):
     hbm = pl.BlockSpec(memory_space=pl.ANY)
     n = len(arrays)
-    sems = pltpu.SemaphoreType.DMA((n, arrays[0].shape[0]))
+    sems = pltpu.SemaphoreType.DMA((n,))
     return pl.pallas_call(
         copy_kernel,
         out_shape=tuple(jax.ShapeDtypeStruct(a.shape, a.dtype) for a in arrays),

time: 216 us -> 214 us (level)
  no operation moved by 1% of the time
where the time goes in v5:
time: 214 us
  Pallas kernels  213 us (100%)
    pallas_call x1, Pallas kernels, local_step(): pl.pallas_call(functools.partial(kernel, n_chip, n_q, d_head ** (-0.5)),...  209 us

profile of v5, /device:TPU:21, one launch (start us, length us, event | category | flops | bytes accessed | tf_op | source)
XLA Modules:
  0.0 213.6 jit_solution(11785000030918206808)
XLA Ops:
  0.6 208.9 %shard_map.75 = (bf16[8,2,512,128]{3,2,1,0:T(8,128)(2,1)}, bf16[8,2,512,128]{3,2,1,0:T(8,128)(2,1)}, bf16[8,256,128]{2,1,0:T(8,128)(2,1)}, bf16[8,256,128]{2,1,0:T(8,128)(2,1)}) custom-call(bf16[8,2,512,128]{3,2,1,0:T(8,128)(2,1)} %bitcast.12, bf16[8,2,512,128]{3,2,1,0:T(8,128)(2,1)} %bitcast.13, bf16[8,256,128]{2,1,0:T(8,128)(2,1)} %bitcast.14, ...), custom_call_target="tpu_custom_call" | custom-call | tf_op jit(solution)/shard_map/pallas_call | solution.py:551
  209.6 4.0 %shard_map.76 = (bf16[8,2,512,128]{3,2,1,0:T(8,128)(2,1)}, bf16[8,2,512,128]{3,2,1,0:T(8,128)(2,1)}, bf16[8,256,128]{2,1,0:T(8,128)(2,1)}, bf16[8,256,128]{2,1,0:T(8,128)(2,1)}) custom-call(bf16[8,2,512,128]{3,2,1,0:T(8,128)(2,1)} %get-tuple-element.12.refs_0_, bf16[8,2,512,128]{3,2,1,0:T(8,128)(2,1)} %get-tuple-element.13.refs_1_, ...), custom_call_target="tpu_custom_call" | custom-call | tf_op jit(solution)/shard_map/pallas_call | solution.py:527

commit v6 on v5

--- a/solution.py
+++ b/solution.py
@@ -13,7 +13,8 @@
 NT = (((1,), (1,)), ((), ()))
 F32 = jnp.float32
 BF16 = jnp.bfloat16
-Q, DO, KV, RELAY, SHARE, O, DQ, FIN, PART, HOME, N_KIND = range(11)
+ROWS, KV, RELAY, SHARE, OUT, FIN, PART, HOME, N_KIND = range(9)
+S_Q, S_DO, S_KV, S_O, S_DQ, S_FIN, N_SELF = range(7)
 H_Q, H_DO, H_K, H_V, H_O, H_DQ, H_FIN, H_PART = range(0, 16, 2)
 
 
@@ -118,15 +119,15 @@
     def own(r, h):
         slot = n_far * r
         b = seq(r, chip)
-        return (pltpu.make_async_copy((k_ref, v_ref)[h].at[b], kv.at[r, h, chip, h], self_sem.at[KV, r]),
-                pltpu.make_async_copy(q_ref.at[b, h], q_in.at[slot, h], self_sem.at[Q, r]),
-                pltpu.make_async_copy(do_ref.at[b, h], do_in.at[slot, h], self_sem.at[DO, r]))
+        return (pltpu.make_async_copy((k_ref, v_ref)[h].at[b], kv.at[r, h, chip, h], self_sem.at[S_KV, r]),
+                pltpu.make_async_copy(q_ref.at[b, h], q_in.at[slot, h], self_sem.at[S_Q, r]),
+                pltpu.make_async_copy(do_ref.at[b, h], do_in.at[slot, h], self_sem.at[S_DO, r]))
 
     def send_rows(d):
         for r in range(2):
             for h in range(2):
-                out_q(r, d, h, q_ref, q_in, Q).start()
-                out_q(r, d, h, do_ref, do_in, DO).start()
+                out_q(r, d, h, q_ref, q_in, ROWS).start()
+                out_q(r, d, h, do_ref, do_in, ROWS).start()
 
     for h in range(2):
         @pl.when(core == h)
@@ -149,8 +150,8 @@
         @pl.when(core == h)
         def _():
             for r in range(2):
-                out_q(r, 0, 1 - h, q_ref, q_in, Q).start()
-                out_q(r, 0, 1 - h, do_ref, do_in, DO).start()
+                out_q(r, 0, 1 - h, q_ref, q_in, ROWS).start()
+                out_q(r, 0, 1 - h, do_ref, do_in, ROWS).start()
             for r in range(2):
                 for cp in own(r, h):
                     cp.wait()
@@ -312,8 +313,7 @@
         for g in range(2):
             @pl.when(jnp.logical_or(d > 0, core != g))
             def _():
-                landed(q_in.at[slot, g], Q, 2 * slot + g).wait_recv()
-                landed(do_in.at[slot, g], DO, 2 * slot + g).wait_recv()
+                landed(q_in.at[slot], ROWS, 2 * slot + g).wait_recv()
 
         def q_rows():
             return q_in[slot].reshape(cols, d_head)
@@ -352,7 +352,7 @@
         for g in range(2):
             @pl.when(jnp.logical_or(d > 0, core != g))
             def _():
-                back(r, d, g, o_st, o_ref.at[seq(r, chip), core], O).start()
+                back(r, d, g, o_st, o_ref.at[seq(r, chip), core], OUT).start()
 
         def backward(j, _):
             p = jnp.exp2(s_buf[j] - lse)
@@ -369,16 +369,16 @@
         for g in range(2):
             @pl.when(jnp.logical_or(d > 0, core != g))
             def _():
-                back(r, d, g, dq_st, dq_ref.at[seq(r, chip), core], DQ).start()
+                back(r, d, g, dq_st, dq_ref.at[seq(r, chip), core], OUT).start()
 
     lax.fori_loop(0, 2 * n_far, tile, 0)
     part_copy(1).start()
 
     def own_out(r, h):
         slot, b = n_far * r, seq(r, chip)
-        return (pltpu.make_async_copy(o_st.at[slot, h], o_ref.at[b, h], self_sem.at[O, r]),
-                pltpu.make_async_copy(dq_st.at[slot, h], dq_ref.at[b, h], self_sem.at[DQ, r]),
-                pltpu.make_async_copy(fin.at[slot, h], (dk_ref, dv_ref)[h].at[b], self_sem.at[FIN, r]))
+        return (pltpu.make_async_copy(o_st.at[slot, h], o_ref.at[b, h], self_sem.at[S_O, r]),
+                pltpu.make_async_copy(dq_st.at[slot, h], dq_ref.at[b, h], self_sem.at[S_DQ, r]),
+                pltpu.make_async_copy(fin.at[slot, h], (dk_ref, dv_ref)[h].at[b], self_sem.at[S_FIN, r]))
 
     for h in range(2):
         @pl.when(core == h)
@@ -477,16 +477,13 @@
 
                 @pl.when(jnp.logical_and(away, leaves(d, chip)))
                 def _():
-                    landed(q_in.at[slot, h], Q, t).wait_send()
-                    landed(do_in.at[slot, h], DO, t).wait_send()
-                    landed(o_ref.at[seq(r, c), h], O, t).wait_recv()
-                    landed(dq_ref.at[seq(r, c), h], DQ, t).wait_recv()
+                    landed(q_in.at[slot], ROWS, t).wait_send()
+                    landed(o_ref.at[seq(r, c)], OUT, t).wait_recv()
                     landed((dk_ref, dv_ref)[h].at[seq(r, c)], FIN, t).wait_recv()
 
                 @pl.when(jnp.logical_and(away, leaves(d, wrap(chip - sign(r) * d))))
                 def _():
-                    landed(o_st.at[slot, h], O, t).wait_send()
-                    landed(dq_st.at[slot, h], DQ, t).wait_send()
+                    landed(o_st.at[slot], OUT, t).wait_send()
                     landed(fin.at[slot, h], FIN, t).wait_send()
 
             @pl.when(stays(d, wrap(chip - sign(r) * d)))
@@ -579,7 +576,7 @@
                 vmem((2, 2, c_len, d_head), BF16),
                 pltpu.SemaphoreType.DMA((N_KIND, n_ctx)),
                 pltpu.SemaphoreType.DMA((N_KIND, n_ctx)),
-                pltpu.SemaphoreType.DMA((N_KIND, 2)),
+                pltpu.SemaphoreType.DMA((N_SELF, 2)),
                 pltpu.SemaphoreType.DMA((16,)),
             ],
             compiler_params=pltpu.CompilerParams(collective_id=0, has_side_effects=True, vmem_limit_bytes=62 * 2 ** 20),

time: 214 us -> 213 us (level)
  no operation moved by 1% of the time
where the time goes in v6:
time: 213 us
  Pallas kernels  212 us (100%)
    pallas_call x1, Pallas kernels, local_step(): pl.pallas_call(functools.partial(kernel, n_chip, n_q, d_head ** (-0.5)),...  208 us

profile of v6, /device:TPU:21, one launch (start us, length us, event | category | flops | bytes accessed | tf_op | source)
XLA Modules:
  0.0 212.7 jit_solution(1143915632091574601)
XLA Ops:
  0.6 208.1 %shard_map.75 = (bf16[8,2,512,128]{3,2,1,0:T(8,128)(2,1)}, bf16[8,2,512,128]{3,2,1,0:T(8,128)(2,1)}, bf16[8,256,128]{2,1,0:T(8,128)(2,1)}, bf16[8,256,128]{2,1,0:T(8,128)(2,1)}) custom-call(bf16[8,2,512,128]{3,2,1,0:T(8,128)(2,1)} %bitcast.12, bf16[8,2,512,128]{3,2,1,0:T(8,128)(2,1)} %bitcast.13, bf16[8,256,128]{2,1,0:T(8,128)(2,1)} %bitcast.14, ...), custom_call_target="tpu_custom_call" | custom-call | tf_op jit(solution)/shard_map/pallas_call | solution.py:548
  208.7 4.0 %shard_map.76 = (bf16[8,2,512,128]{3,2,1,0:T(8,128)(2,1)}, bf16[8,2,512,128]{3,2,1,0:T(8,128)(2,1)}, bf16[8,256,128]{2,1,0:T(8,128)(2,1)}, bf16[8,256,128]{2,1,0:T(8,128)(2,1)}) custom-call(bf16[8,2,512,128]{3,2,1,0:T(8,128)(2,1)} %get-tuple-element.12.refs_0_, bf16[8,2,512,128]{3,2,1,0:T(8,128)(2,1)} %get-tuple-element.13.refs_1_, ...), custom_call_target="tpu_custom_call" | custom-call | tf_op jit(solution)/shard_map/pallas_call | solution.py:524
